TPU v7x, 512 devices: a 4x2x32 block of a 4x8x32 slice. The times are simulated.
512 devices in a mesh: rep: 2 (over y), gx: 128 (over x, z), gy: 2 (over core).
Axes of the slice: x: 4, y: 2, z: 32, core: 2. Of those that a mesh axis runs over, the one named last changes fastest.
The devices are a block of a 4x8x32 slice.
Arguments:
- tokens: bfloat16 [768, 8192], P(('rep', 'gx'), 'gy'), parts along dimension 0, may hold values from -6 to 6
- segment_ids: int32 [768], P(('rep', 'gx')), parts along dimension 0, may hold values from 0 to 1, as said below
- gate_weight: bfloat16 [8192, 2, 13312], P(None, 'gy', 'gx'), may hold values from -0.0625 to 0.0625
- up_weight: bfloat16 [8192, 2, 13312], P(None, 'gy', 'gx'), may hold values from -0.0625 to 0.0625
- down_weight: bfloat16 [2, 13312, 8192], P('gy', None, 'gx'), may hold values from -0.0390625 to 0.0390625
Outputs:
- grouped: bfloat16 [768, 8192], P(('rep', 'gx'), 'gy'), parts along dimension 0
There are 2 independent parts, one for each index of `rep`. A program takes and returns all parts, laid end to end along the dimension named above; an argument that names none is the same for every part. Nothing has to cross between parts.
Inputs may be any that keep to these rules, and one draw needn't show every extreme that they name: `segment_ids`: exactly 320 entries are 0 and 64 entries are 1.
All inputs are finite; a program needn't handle non-finite values.
Results may differ from a plain program's by a relative error of at most 0.0049.
Values may be sent and summed in bfloat16 or wider, within the bound.
No kernel may reach another device: no remote copies, remote signals or barrier semaphores. Data moves between devices by JAX's collectives and lax.ppermute only.
A program may use at most 128 MiB of HBM per device.

v0:
```python
import jax
import jax.numpy as jnp
from jax import lax
from jax.sharding import Mesh
from jax.sharding import PartitionSpec as P

PREFILL = 320
GX = ("gx_0", "gx_1")
REP_GX = ("rep", "gx_0", "gx_1")


def gather_axes(shard, axes, dim):
    for axis in reversed(axes):
        shard = lax.all_gather(shard, axis, axis=dim, tiled=True)
    return shard


def from_everyone(shard, axis):
    copies = jnp.broadcast_to(shard, (lax.axis_size(axis), *shard.shape))
    return lax.all_to_all(copies, axis, split_axis=0, concat_axis=0, tiled=True)


def laid_out(blocks, dim):
    dims = list(blocks.shape[1:])
    dims[dim] *= blocks.shape[0]
    return jnp.moveaxis(blocks, 0, dim).reshape(dims)


def gathered_copies(shard, axis, dim):
    blocks = from_everyone(shard, axis)
    return laid_out(blocks, dim)


def all_blocks(shard, axes, sequence):
    blocks = shard[None]
    for k in sequence:
        blocks = lax.all_gather(blocks, axes[k], axis=0, tiled=True)
    current = [lax.axis_size(axes[k]) for k in reversed(sequence)]
    blocks = blocks.reshape(*current, *shard.shape)
    turned = sorted(range(len(sequence)), key=lambda place: sequence[len(sequence) - 1 - place])
    return blocks.transpose(*turned, *range(len(sequence), blocks.ndim)).reshape(-1, *shard.shape)


def gather_axes_2(shard, axes, sequence, dim):
    return laid_out(all_blocks(shard, axes, sequence), dim)


def cut_along(shard, dim, count):
    before, after = (shard.shape[:dim], shard.shape[dim + 1 :])
    return jnp.moveaxis(shard.reshape(*before, count, -1, *after), dim, 0)


def summed_on_arrival(shard, axis, dim):
    count = lax.axis_size(axis)
    blocks = lax.all_to_all(cut_along(shard, dim, count), axis, 0, 0, tiled=True)
    return jnp.sum(blocks, axis=0)


def grouped_target(token_kinds):
    decode_flag = token_kinds.astype(jnp.int32)
    prefill_flag = 1 - decode_flag
    prefill_rank = jnp.cumsum(prefill_flag) - 1
    decode_rank = jnp.cumsum(decode_flag) - 1
    return jnp.where(decode_flag == 0, prefill_rank, PREFILL + decode_rank)


def local(tokens, segment_ids, gate_weight, up_weight, down_weight):
    half_rows, token_kinds = (gather_axes(tokens, GX, 0), gather_axes(segment_ids, GX, 0))
    gathered = gathered_copies(half_rows, "gy", 1)
    gate_local = gate_weight.reshape(gate_weight.shape[0], -1)
    up_local = up_weight.reshape(up_weight.shape[0], -1)
    down_local = down_weight.reshape(-1, down_weight.shape[2])
    target = grouped_target(token_kinds)
    gate_value = jnp.dot(gathered, gate_local, preferred_element_type=jnp.float32)
    up_value = jnp.dot(gathered, up_local, preferred_element_type=jnp.float32)
    hidden = (jax.nn.silu(gate_value) * up_value).astype(jnp.bfloat16)
    partial_value = jnp.dot(
        gather_axes_2(hidden, GX, (0, 1), 1), down_local, preferred_element_type=jnp.float32
    )
    placed = jnp.zeros_like(partial_value).at[target].set(partial_value)
    switched = lax.all_to_all(placed, GX, split_axis=0, concat_axis=1, tiled=True)
    return summed_on_arrival(switched, "gy", 1).astype(jnp.bfloat16)


def solution(mesh):
    torus = Mesh(
        mesh.devices.reshape(mesh.shape["rep"], 4, 32, mesh.shape["gy"]),
        ("rep", "gx_0", "gx_1", "gy"),
    )
    placed = (P(REP_GX, "gy"), P(REP_GX), P(None, "gy", GX), P(None, "gy", GX), P("gy", None, GX))
    return jax.shard_map(
        local, mesh=torus, in_specs=placed, out_specs=P(REP_GX, "gy"), check_vma=False
    )
```

profile of v0, /device:TPU:33, one launch (start us, length us, event | category | flops | bytes accessed | tf_op | source)
XLA Modules:
  0.0 413.4 jit_solution(14316246672419341581)
XLA Ops:
  6.6 88.2 %all-gather.1 = bf16[32,3,4096]{2,1,0:T(4,128)(2,1)S(1)} all-gather(bf16[1,3,4096]{2,1,0:T(4,128)(2,1)} %bitcast.53), channel_id=1, replica_groups=mesh['rep'=2,'gx_0'=4,'gx_1'=32,'gy'=2] {'gx_1'}, dimensions={0}, use_global_device_ids=true | all-gather | bytes 811008 | tf_op jit(solution)/shard_map/all_gather | solution.py:14
  94.7 1.4 reshape.89
  96.3 53.2 %all-gather.5.cloned.1.call-done = bf16[384,4096]{1,0:T(8,128)(2,1)} async-done(((bf16[96,4096]{1,0:T(8,128)(2,1)}), bf16[384,4096]{1,0:T(8,128)(2,1)}) %all-gather.5.cloned.1.call-update) | async-done | bytes 3145744 | tf_op jit(solution)/shard_map/all_gather | solution.py:14
  149.5 4.7 %copy.14 = bf16[384,4096]{0,1:T(8,128)(2,1)} copy(bf16[384,4096]{1,0:T(8,128)(2,1)} %all-gather.5.cloned.1.call-done) | data formatting | bytes 6291456 | tf_op jit(solution)/shard_map/all_gather | solution.py:14
  154.2 2.4 broadcast_in_dim.14
  156.6 9.3 %all_to_all.26 = bf16[2,384,4096]{1,2,0:T(8,128)(2,1)S(1)} all-to-all(bf16[2,384,4096]{1,2,0:T(8,128)(2,1)S(1)} %broadcast_in_dim.14), channel_id=1, replica_groups=mesh['rep'=2,'gx_0'=4,'gx_1'=32,'gy'=2] {'gy'}, dimensions={0} | all-to-all | bytes 12582912 | tf_op jit(solution)/shard_map/all_to_all | solution.py:20
  165.9 1.2 fusion.4
  167.3 1.2 fusion.9
  168.5 9.7 %all-gather = bf16[1536,104]{0,1:T(8,128)(2,1)S(1)} all-gather(bf16[384,104]{0,1:T(8,128)(2,1)S(1)} %fusion.9), channel_id=2, replica_groups=mesh['rep'=2,'gx_0'=4,'gx_1'=32,'gy'=2] {'gx_0'}, dimensions={0}, use_global_device_ids=true | all-gather | bytes 399360 | tf_op jit(solution)/shard_map/all_gather | solution.py:37
  178.2 0.7 copy.23
  179.0 1.3 dynamic-slice
  180.3 1.3 dynamic-slice.1
  183.1 33.9 %all-reduce = s32[96]{0:T(128)S(1)} all-reduce(s32[96]{0:T(128)S(1)} %dynamic-update-slice), channel_id=1, replica_groups=mesh['rep'=2,'gx_0'=4,'gx_1'=32,'gy'=2] {'gx_1'}, use_global_device_ids=true, to_apply=%add | all-reduce | flops 96 | bytes 768
  217.2 5.6 %all-reduce.1 = s32[384]{0:T(512)S(1)} all-reduce(s32[384]{0:T(512)S(1)} %dynamic-update-slice.1), channel_id=1, replica_groups=mesh['rep'=2,'gx_0'=4,'gx_1'=32,'gy'=2] {'gx_0'}, use_global_device_ids=true, to_apply=%add.1 | all-reduce | flops 384 | bytes 3072
  222.8 0.3 reduce-window.16
  223.9 96.5 %all-gather.7.cloned.1.call-done = bf16[128,384,104]{1,2,0:T(8,128)(2,1)} async-done(((bf16[4,384,104]{1,2,0:T(8,128)(2,1)}), bf16[128,384,104]{1,2,0:T(8,128)(2,1)}) %all-gather.7.cloned.1.call-update) | async-done | bytes 10223632 | tf_op jit(solution)/shard_map/all_gather | solution.py:37
  320.3 8.9 %copy.16 = bf16[4,32,384,104]{2,3,1,0:T(8,128)(2,1)} copy(bf16[4,32,384,104]{2,3,0,1:T(8,128)(2,1)} %bitcast.47) | data formatting | bytes 20447232 | tf_op jit(solution)/shard_map/transpose | solution.py:41
  329.2 6.2 %fusion = f32[384,64]{1,0:T(8,128)} fusion(bf16[384,13312]{0,1:T(8,128)(2,1)} %bitcast.48, bf16[1,13312,64]{1,2,0:T(8,128)(2,1)S(1)} %copy-done.2), kind=kOutput, calls=%fused_computation.1 | convolution fusion | flops 654311424 | bytes 12025856 | tf_op jit(solution)/shard_map/dot_general | solution.py:77
  335.4 1.9 scatter_custom_fusion
  337.6 45.1 %all_to_all.27 = f32[128,1,192]{2,1,0:T(1,128)S(1)} all-to-all(f32[128,1,192]{2,1,0:T(1,128)S(1)} %reshape.98), channel_id=1, replica_groups=mesh['rep'=2,'gx_0'=4,'gx_1'=32,'gy'=2] {'gx_0','gx_1'}, dimensions={0} | all-to-all | bytes 196608 | tf_op jit(solution)/shard_map/all_to_all | solution.py:81
  382.7 0.5 broadcast.39
  383.2 1.0 reduce.4
  384.6 21.4 %all_to_all.28 = f32[2,3,4096]{2,1,0:T(4,128)S(1)} all-to-all(f32[2,3,4096]{2,1,0:T(4,128)S(1)} %copy.19), channel_id=1, replica_groups=mesh['rep'=2,'gx_0'=4,'gx_1'=32,'gy'=2] {'gy'}, dimensions={0} | all-to-all | bytes 196608 | tf_op jit(solution)/shard_map/all_to_all | solution.py:55
  405.9 0.6 reduce_sum.9
  (30 shorter events, 2.3 us)
Async XLA Ops:
  6.5 159.3 %copy-start = (bf16[8192,1,104]{0,2,1:T(8,128)(2,1)S(1)}, bf16[8192,1,104]{0,2,1:T(8,128)(2,1)}, u32[]{:S(2)}) copy-start(bf16[8192,1,104]{0,2,1:T(8,128)(2,1)} %param.7) | copy-start | bytes 5111812
  6.6 142.9 %all-gather.5.cloned.1.call-start = ((), (), s32[]{:S(2)}) async-start(), calls=%async_computation.3 | async-start | bytes 3932160 | tf_op jit(solution)/shard_map/all_gather | solution.py:14
  96.2 224.2 %all-gather.7.cloned.1.call-start = ((), (), s32[]{:S(2)}) async-start(), calls=%async_computation.4 | async-start | bytes 10543104 | tf_op jit(solution)/shard_map/all_gather | solution.py:37
  165.9 1.5 copy-start.1
  167.3 15.6 %copy-start.3 = (s32[3]{0:T(128)S(1)}, s32[3]{0:T(128)}, u32[]{:S(2)}) copy-start(s32[3]{0:T(128)} %param.6) | copy-start | bytes 40
  320.3 8.9 %copy-start.2 = (bf16[1,13312,64]{1,2,0:T(8,128)(2,1)S(1)}, bf16[1,13312,64]{1,2,0:T(8,128)(2,1)}, u32[]{:S(2)}) copy-start(bf16[1,13312,64]{1,2,0:T(8,128)(2,1)} %param.9) | copy-start | bytes 5111812
Sparse Core Ops, SparseCore 0:
  96.3 53.1 all-gather.4
  179.1 141.1 all-gather.6
where the time goes:
time: 414 us; the launch traced here: 413 us
  blocking collectives  213 us (51%)
  waiting for transfers between devices  150 us (36%)
  local copies, waits for them, and re-layouts  24.7 us (6%)
  between operations  14.8 us (4%)
  matrix products  8.6 us (2%)
    all_gather x1, waiting for transfers between devices, all_blocks(): blocks = lax.all_gather(blocks, axes[k], axis=0, tiled=True)  96.5 us
    all_gather x1, blocking collectives, gather_axes(): shard = lax.all_gather(shard, axis, axis=dim, tiled=True)  88.2 us
    all_gather x1, waiting for transfers between devices, gather_axes(): shard = lax.all_gather(shard, axis, axis=dim, tiled=True)  53.2 us
    all_to_all x1, blocking collectives, local(): lax.all_to_all(placed, GX, split_axis=0, concat_axis=1, tiled=True)  45.1 us
    unnamed x2, blocking collectives  39.5 us
    all_to_all x1, blocking collectives, summed_on_arrival(): lax.all_to_all(cut_along(shard, dim, count), axis, 0, 0, tiled=True)  21.4 us
    all_gather x1, blocking collectives, all_blocks(): blocks = lax.all_gather(blocks, axes[k], axis=0, tiled=True)  9.68 us
    all_to_all x1, blocking collectives, from_everyone(): return lax.all_to_all(copies, axis, split_axis=0, concat_axis=0, tiled=True)  9.27 us
  transfers between devices with their start and end apart: 2, of which 2 were waited for; matrix products, arithmetic and copies ran while one was open for 1% of the time, Pallas kernels for 0%

commit v1 on v0

--- a/solution.py
+++ b/solution.py
@@ -34,7 +34,9 @@
 def all_blocks(shard, axes, sequence):
     blocks = shard[None]
     for k in sequence:
-        blocks = lax.all_gather(blocks, axes[k], axis=0, tiled=True)
+        blocks = jnp.concatenate(
+            lax.all_to_all(jnp.stack([blocks] * lax.axis_size(axes[k])), axes[k], 0, 0), axis=0
+        )
     current = [lax.axis_size(axes[k]) for k in reversed(sequence)]
     blocks = blocks.reshape(*current, *shard.shape)
     turned = sorted(range(len(sequence)), key=lambda place: sequence[len(sequence) - 1 - place])

time: 414 us -> 1200 us (2.90)
  blocking collectives: 213 us -> 1070 us
  waiting for transfers between devices: 150 us -> 53.3 us
  starting transfers between devices: 0.07 us -> 23.3 us
    unnamed x2, blocking collectives: 39.5 us -> 900 us
    all_gather x1 -> x0, waiting for transfers between devices: 96.5 us -> none  [all_blocks(): blocks = lax.all_gather(blocks, axes[k], axis=0, tiled=True)]
    all_to_all x0 -> x1, starting transfers between devices: none -> 23.3 us  [all_blocks(): lax.all_to_all(jnp.stack([blocks] * lax.axis_size(axes[k])), axes[k], 0, 0)]
  transfers between devices with their start and end apart: 2 -> 2, of which waited for: 2 -> 1; matrix products, arithmetic and copies ran while one was open for 1% -> 0% of each run, Pallas kernels for 0% -> 0%
where the time goes in v1:
time: 1200 us
  blocking collectives  1070 us (89%)
  waiting for transfers between devices  53.3 us (4%)
  local copies, waits for them, and re-layouts  29 us (2%)
  starting transfers between devices  23.3 us (2%)
  between operations  14.9 us (1%)
    unnamed x2, blocking collectives  900 us
    all_gather x1, blocking collectives, gather_axes(): shard = lax.all_gather(shard, axis, axis=dim, tiled=True)  88.2 us
    all_to_all x1, blocking collectives, local(): lax.all_to_all(placed, GX, split_axis=0, concat_axis=1, tiled=True)  54.5 us
    all_gather x1, waiting for transfers between devices, gather_axes(): shard = lax.all_gather(shard, axis, axis=dim, tiled=True)  53.3 us
  transfers between devices with their start and end apart: 2, of which 1 were waited for; matrix products, arithmetic and copies ran while one was open for 0% of the time, Pallas kernels for 0%

profile of v1, /device:TPU:33, one launch (start us, length us, event | category | flops | bytes accessed | tf_op | source)
XLA Modules:
  0.0 1202.8 jit_solution(11869476464979512778)
XLA Ops:
  6.6 88.2 %all-gather = bf16[32,3,4096]{2,1,0:T(4,128)(2,1)S(1)} all-gather(bf16[1,3,4096]{2,1,0:T(4,128)(2,1)} %bitcast.47), channel_id=1, replica_groups=mesh['rep'=2,'gx_0'=4,'gx_1'=32,'gy'=2] {'gx_1'}, dimensions={0}, use_global_device_ids=true | all-gather | bytes 811008 | tf_op jit(solution)/shard_map/all_gather | solution.py:14
  94.7 1.4 reshape.88
  96.2 53.3 %all-gather.3.cloned.1.call-done = bf16[384,4096]{1,0:T(8,128)(2,1)} async-done(((bf16[96,4096]{1,0:T(8,128)(2,1)}), bf16[384,4096]{1,0:T(8,128)(2,1)}) %all-gather.3.cloned.1.call-update) | async-done | bytes 3145744 | tf_op jit(solution)/shard_map/all_gather | solution.py:14
  149.5 4.7 copy.10
  154.2 2.4 broadcast_in_dim.11
  156.6 9.3 all_to_all.36
  165.9 1.2 fusion.4
  167.3 1.2 fusion.9
  168.6 9.4 all_to_all.37
  178.0 4.7 stack.7
  182.7 23.3 %all-to-all-start.2 = ((bf16[32,4,384,104]{2,3,1,0:T(8,128)(2,1)}), bf16[32,4,384,104]{2,3,1,0:T(8,128)(2,1)}, u32[]{:S(2)}, u32[]{:S(2)}) async-start(bf16[32,4,384,104]{2,3,1,0:T(8,128)(2,1)} %stack.7), calls=%async_computation.2 | async-start | bytes 20447232 | tf_op jit(solution)/shard_map/all_to_all | solution.py:38
  206.1 1.3 dynamic-slice
  207.3 1.3 dynamic-slice.1
  210.3 894.9 %all-reduce = s32[96]{0:T(128)S(1)} all-reduce(s32[96]{0:T(128)S(1)} %dynamic-update-slice), channel_id=1, replica_groups=mesh['rep'=2,'gx_0'=4,'gx_1'=32,'gy'=2] {'gx_1'}, use_global_device_ids=true, to_apply=%add | all-reduce | flops 96 | bytes 768
  1105.4 4.8 all-reduce.1
  1110.1 0.3 reduce-window.16
  1111.2 8.9 copy.11
  1120.1 6.2 fusion
  1126.3 2.0 scatter_custom_fusion
  1128.7 54.5 %all_to_all.38 = f32[128,1,192]{2,1,0:T(1,128)S(1)} all-to-all(f32[128,1,192]{2,1,0:T(1,128)S(1)} %reshape.97), channel_id=1, replica_groups=mesh['rep'=2,'gx_0'=4,'gx_1'=32,'gy'=2] {'gx_0','gx_1'}, dimensions={0} | all-to-all | bytes 196608 | tf_op jit(solution)/shard_map/all_to_all | solution.py:83
  1183.2 0.5 broadcast.42
  1183.7 1.0 reduce.4
  1185.1 10.3 all_to_all.39
  1195.3 0.6 reduce_sum.9
  (30 shorter events, 2.2 us)
Async XLA Ops:
  6.5 159.3 %copy-start = (bf16[8192,1,104]{0,2,1:T(8,128)(2,1)S(1)}, bf16[8192,1,104]{0,2,1:T(8,128)(2,1)}, u32[]{:S(2)}) copy-start(bf16[8192,1,104]{0,2,1:T(8,128)(2,1)} %param.7) | copy-start | bytes 5111812
  6.6 142.9 %all-gather.3.cloned.1.call-start = ((), (), s32[]{:S(2)}) async-start(), calls=%async_computation.5 | async-start | bytes 3932160 | tf_op jit(solution)/shard_map/all_gather | solution.py:14
  165.9 1.5 copy-start.1
  182.7 27.3 %copy-start.3 = (s32[3]{0:T(128)S(1)}, s32[3]{0:T(128)}, u32[]{:S(2)}) copy-start(s32[3]{0:T(128)} %param.6) | copy-start | bytes 40
  182.7 928.5 %all-to-all-start.2 = ((bf16[32,4,384,104]{2,3,1,0:T(8,128)(2,1)}), bf16[32,4,384,104]{2,3,1,0:T(8,128)(2,1)}, u32[]{:S(2)}, u32[]{:S(2)}) async-start(bf16[32,4,384,104]{2,3,1,0:T(8,128)(2,1)} %stack.7), calls=%async_computation.2 | async-start | bytes 20447232 | tf_op jit(solution)/shard_map/all_to_all | solution.py:38
  1111.2 8.9 copy-start.2
Sparse Core Ops, SparseCore 0:
  96.3 53.1 all-gather.2
